TPU v7x, 32 devices: a whole 2x2x4 slice. The times are simulated.
32 devices in a mesh: gx: 4 (over y, x), gy: 8 (over z, core).
Axes of the slice: x: 2, y: 2, z: 4, core: 2. Of those that a mesh axis runs over, the one named last changes fastest.
Arguments:
- u_wind: float32 [64, 64, 1024], P(None, 'gx', 'gy'), may hold values from -6 to 6
- v_wind: float32 [64, 64, 1024], P(None, 'gx', 'gy'), may hold values from -6 to 6
- w_wind: float32 [64, 64, 1024], P(None, 'gx', 'gy'), may hold values from -4 to 4
- pressure: float32 [64, 64, 1024], P(None, 'gx', 'gy'), may hold values from -6 to 6
- terrain_level: int32 [64, 1024], P('gx', 'gy'), may hold values from 0 to 8
- zone_width: int32 [4], replicated, may hold values from 5 to 16
- stiffness: float32 [64], replicated, may hold values from 0.25 to 2
- inflow_profile: float32 [2, 64], replicated, may hold values from -5 to 5
Outputs:
- u_final: float32 [64, 64, 1024], P(None, 'gx', 'gy')
- v_final: float32 [64, 64, 1024], P(None, 'gx', 'gy')
- w_final: float32 [64, 64, 1024], P(None, 'gx', 'gy')
- p_final: float32 [64, 64, 1024], P(None, 'gx', 'gy')
Inputs may be any that keep to these rules, and one draw needn't show every extreme that they name: `zone_width`: zone widths in columns.
All inputs are finite; a program needn't handle non-finite values.
Results may differ from a plain program's by a relative error of at most 0.0001.
Values sent between devices are 32-bit elements; how exact they have to be, the bound alone decides.
A program may use at most 128 MiB of HBM per device.

v0:
```python
import functools

import jax
import jax.numpy as jnp
from jax import lax
from jax.experimental import pallas as pl
from jax.experimental.pallas import tpu as pltpu
from jax.sharding import PartitionSpec as P

SUB = 6
ADV = 0.3
HC = 0.4
ZC = 1.0
RELAX = 0.5
TERRAIN_MAX = 8
DRY = 1 << 20
WEST, EAST, SOUTH, NORTH = 0, 1, 2, 3
FU, FP, FV, FW = 0, 1, 2, 3
LO = 8
ROWS = 40
PEXT = 32
GROUP = 16
HALF = 32
CENT = {-3: 1.0, -2: -8.0, -1: 37.0, 0: 37.0, 1: -8.0, 2: 1.0}
UPW = {-3: -1.0, -2: 5.0, -1: -10.0, 0: 10.0, 1: -5.0, 2: 1.0}


def stencil(c, m3, m2, m1, f0, e1, e2):
    centered = 37.0 * (f0 + m1) - 8.0 * (e1 + m2) + (e2 + m3)
    upwind = 10.0 * (f0 - m1) - 5.0 * (e1 - m2) + (e2 - m3)
    return c * centered - jnp.abs(c) * upwind


def weights(dist, table):
    out = jnp.zeros(dist.shape, jnp.float32)
    for off, value in table.items():
        out = jnp.where(dist == off, value, out)
    return out.astype(jnp.bfloat16)


def split(x):
    hi = x.astype(jnp.bfloat16)
    return hi, (x - hi.astype(jnp.float32)).astype(jnp.bfloat16)


def kernel(
    nz,
    bx,
    cnt,
    u_in,
    v_in,
    w_in,
    p_in,
    terr,
    zone,
    g,
    prof,
    u_out,
    v_out,
    w_out,
    p_out,
    raw,
    tend,
    pres,
    wsc,
    q_buf,
    d_buf,
    cc,
    li,
    wi,
    lhs,
    mat,
    mat_c,
    prod,
    c_next,
    ys,
    yr,
    trx,
    tr_y,
    pw_r,
    pe_r,
    ps_y,
    pr_y,
    uh_x,
    vs_y,
    vr_y,
    ub_x,
    gh_x,
    wet_x,
    in_s,
    ini_s,
    ini_r,
    iny_s,
    iny_r,
    ter_s,
    ter_r,
    uv_s,
    uv_r,
    stp_s,
    stp_r,
):
    by = 128
    nkg = nz // GROUP
    nh = nz // HALF
    gx = lax.axis_index("gx")
    gy = lax.axis_index("gy")
    nx_dev, ny_dev = cnt
    has = (gx > 0, gx < nx_dev - 1, gy > 0, gy < ny_dev - 1)
    peer = ({"gx": gx - 1}, {"gx": gx + 1}, {"gy": gy - 1}, {"gy": gy + 1})
    opp = (EAST, WEST, NORTH, SOUTH)

    loads = [
        pltpu.make_async_copy(src, raw.at[f, :, pl.ds(LO, bx), :], in_s.at[f])
        for f, src in ((FU, u_in), (FP, p_in), (FV, v_in), (FW, w_in))
    ]
    for c in loads:
        c.start()

    barrier = pltpu.get_barrier_semaphore()
    for d in range(4):

        @pl.when(has[d])
        def _(d=d):
            pl.semaphore_signal(
                barrier, inc=1, device_id=peer[d], device_id_type=pl.DeviceIdType.MESH
            )

    def rcopy(d, src, dst, ss, rs):
        return pltpu.make_async_remote_copy(
            src_ref=src,
            dst_ref=dst,
            send_sem=ss,
            recv_sem=rs,
            device_id=peer[d],
            device_id_type=pl.DeviceIdType.MESH,
        )

    def start(d, *copies):
        @pl.when(has[d])
        def _():
            for c in copies:
                rcopy(d, *c).start()

    def wait_send(d, *copies):
        @pl.when(has[d])
        def _():
            for c in copies:
                rcopy(d, *c).wait_send()

    def wait_recv(d, *copies):
        @pl.when(has[opp[d]])
        def _():
            for c in copies:
                rcopy(d, *c).wait_recv()

    def ini(d, grp, c):
        out = []
        for r in range(3):
            own = LO + r if d == WEST else LO + bx - 3 + r
            far = LO + bx + r if d == WEST else LO - 3 + r
            f = pl.ds(2 * grp, 2)
            k = pl.ds(c * GROUP, GROUP)
            out.append(
                (
                    raw.at[f, k, own, :],
                    raw.at[f, k, far, :],
                    ini_s.at[d, grp, c, r],
                    ini_r.at[d, grp, c, r],
                )
            )
        return out

    def iny(d, c):
        return ys.at[c], yr.at[d - 2, c], iny_s.at[d - 2, c], iny_r.at[d - 2, c]

    def ter(d):
        if d == WEST:
            return terr.at[pl.ds(0, 8)], trx, ter_s.at[0], ter_r.at[0]
        return terr, tr_y, ter_s.at[1], ter_r.at[1]

    def uvx(h):
        k = pl.ds(h * HALF, HALF)
        return u_out.at[k, 0, :], uh_x.at[k], uv_s.at[h], uv_r.at[h]

    def uvy():
        return vs_y, vr_y, uv_s.at[nh], uv_r.at[nh]

    def stp(d, s, h=0):
        sems = stp_s.at[d, s, h], stp_r.at[d, s, h]
        if d < 2:
            k = pl.ds(h * HALF, HALF)
            row = LO if d == WEST else LO + bx - 1
            return pres.at[k, row, :], (pe_r, pw_r)[d].at[s, k], *sems
        return ps_y.at[s], pr_y.at[d - 2, s], *sems

    rows = lax.broadcasted_iota(jnp.int32, (bx, by), 0)
    lane = lax.broadcasted_iota(jnp.int32, (bx, by), 1)
    zero = jnp.zeros((bx, by), jnp.float32)

    def slab(k):
        return pl.ds(pl.multiple_of(k * bx, bx), bx)

    zrow = jnp.zeros((8, by), jnp.float32)

    def clear(k, carry):
        pres[k, pl.ds(0, 8), :] = zrow
        return carry

    lax.fori_loop(0, nz, clear, 0, unroll=8)

    for d in range(4):

        @pl.when(jnp.logical_not(has[opp[d]]))
        def _(d=d):
            if d == WEST:
                pe_r[...] = jnp.zeros(pe_r.shape, jnp.float32)
                uh_x[...] = jnp.zeros(uh_x.shape, jnp.float32)
                trx[...] = jnp.full(trx.shape, DRY, jnp.int32)
            if d == EAST:
                pw_r[...] = jnp.zeros(pw_r.shape, jnp.float32)
            if d < 2:
                at = pl.ds(LO + bx if d == WEST else 0, 8)

                def blank(k, carry):
                    for f in range(4):
                        raw[f, k, at, :] = zrow
                    return carry

                lax.fori_loop(0, nz, blank, 0, unroll=4)
            else:
                yr[d - 2] = jnp.zeros(yr.shape[1:], jnp.float32)
                pr_y[d - 2] = jnp.zeros(pr_y.shape[1:], jnp.float32)
            if d == SOUTH:
                tr_y[...] = jnp.full(tr_y.shape, DRY, jnp.int32)
                vr_y[...] = jnp.zeros(vr_y.shape, jnp.float32)

    loads[0].wait()
    loads[1].wait()
    pl.semaphore_wait(barrier, sum(h.astype(jnp.int32) for h in has))
    start(WEST, *[x for c in range(nkg) for x in ini(WEST, 0, c)])
    start(EAST, *[x for c in range(nkg) for x in ini(EAST, 0, c)])
    start(WEST, ter(WEST))
    start(SOUTH, ter(SOUTH))
    loads[2].wait()
    loads[3].wait()
    start(WEST, *[x for c in range(nkg) for x in ini(WEST, 1, c)])
    start(EAST, *[x for c in range(nkg) for x in ini(EAST, 1, c)])

    def pack(kg, carry):
        for f in range(4):
            acc = zero
            for kk in range(GROUP):
                x = raw[f, kg * GROUP + kk, pl.ds(LO, bx), :]
                acc = jnp.where((lane >> 3) == kk, pltpu.roll(x, 8 * kk + 3, 1), acc)
            ys[kg, f] = acc
        start(SOUTH, iny(SOUTH, kg))
        start(NORTH, iny(NORTH, kg))
        return carry

    lax.fori_loop(0, nkg, pack, 0)

    sq_r = lax.broadcasted_iota(jnp.int32, (by, by), 0)
    sq_c = lax.broadcasted_iota(jnp.int32, (by, by), 1)
    part = sq_r & 7
    far = jnp.where(part < 3, part - 3, jnp.where(part < 6, by - 3 + part, 8 * by))
    for src, at in ((sq_r, 0), (far, 2 * by)):
        for n in range(4):
            w = weights(src - sq_c - n // 2, (CENT, UPW)[n % 2])
            mat[pl.ds(at, by), pl.ds(n * by, by)] = w
            mat[pl.ds(at + by, by), pl.ds(n * by, by)] = w
        w = weights(src - sq_c - 1, {0: 1.0})
        mat_c[pl.ds(at, by), :] = w
        mat_c[pl.ds(at + by, by), :] = w

    def relax_of(ci, rj):
        best = None
        for n, dist in enumerate(
            (ci, (nx_dev * bx - 1.0) - ci, rj, (ny_dev * by - 1.0) - rj)
        ):
            width = jnp.full(ci.shape, zone[n], jnp.int32).astype(jnp.float32)
            ramp = jnp.maximum(width - dist, 0.0) / width
            best = ramp if best is None else jnp.maximum(best, ramp)
        return RELAX * best

    start_x = gx * bx
    start_y = gy * by
    ci = (rows + start_x).astype(jnp.float32)
    rj = (lane + start_y).astype(jnp.float32)
    relax = relax_of(ci, rj)
    keep = 1.0 - relax
    relax_hx = relax_of(
        (jnp.zeros((8, by), jnp.int32) + (start_x + bx)).astype(jnp.float32), rj[:8]
    )
    relax_hy = relax_of(ci, (jnp.zeros((bx, by), jnp.int32) + (start_y + by)).astype(jnp.float32))

    t0 = terr[...]

    def coeff(k, carry):
        c_prev, vrow = carry
        wet = t0 <= k
        gk = (ZC * ZC) * g[k]
        ga = (ZC * ZC) * jnp.where(k + 1 < nz, g[jnp.minimum(k + 1, nz - 1)], 0.0)
        inv = jnp.where(wet, 1.0 / (1.0 + ((ga + gk) - gk * c_prev)), 0.0)
        c_new = ga * inv
        wi[slab(k), :] = inv
        li[slab(k), :] = gk * inv
        cc[slab(k), :] = c_new
        ub_x[pl.ds(k, 1), :] = jnp.full((1, by), prof[0, k], jnp.float32)
        gh_x[pl.ds(k, 1), :] = jnp.full((1, by), g[k] * (HC * HC), jnp.float32)
        vrow = jnp.where((lane >> 1) == k, prof[1, k], vrow)
        return c_new, vrow

    _, vb_y = lax.fori_loop(0, nz, coeff, (zero, zero))

    wait_recv(WEST, ter(WEST))
    wait_recv(SOUTH, ter(SOUTH))
    sub8 = lax.broadcasted_iota(jnp.int32, (8, by), 0)
    t_east = jnp.broadcast_to(trx[0:1, :], (8, by))
    for k in range(0, nz, 8):
        wet_x[pl.ds(k, 8), :] = jnp.where(t_east <= sub8 + k, 1.0, 0.0)
    t_north = jnp.broadcast_to(tr_y[:, 0:1], (bx, by))
    wet_y = jnp.where(t_north <= (lane >> 1), 1.0, 0.0)

    scale = ADV / 60.0

    def along_y(kg, carry):
        wait_recv(SOUTH, iny(SOUTH, kg))
        wait_recv(NORTH, iny(NORTH, kg))
        for f in (FV, FU, FP, FW):
            halo = split(
                jnp.where((lane & 7) < 3, yr[NORTH - 2, kg, f], yr[SOUTH - 2, kg, f])
            )
            for kk in range(GROUP):
                at = pl.ds(kk * bx, bx)
                hi, lo = split(raw[f, kg * GROUP + kk, pl.ds(LO, bx), :])
                lhs[at, pl.ds(0, by)] = hi
                lhs[at, pl.ds(by, by)] = lo
                mine = (lane >> 3) == kk
                for n in range(2):
                    lhs[at, pl.ds((2 + n) * by, by)] = jnp.where(mine, halo[n], 0.0).astype(
                        jnp.bfloat16
                    )
            if f == FV:
                c_next[...] = scale * jnp.dot(
                    lhs[...], mat_c[...], preferred_element_type=jnp.float32
                )
            prod[...] = jnp.dot(lhs[...], mat[...], preferred_element_type=jnp.float32)
            for kk in range(GROUP):
                at = pl.ds(kk * bx, bx)
                k = kg * GROUP + kk
                c0 = raw[FV, k, pl.ds(LO, bx), :] * scale
                c1 = c_next[at, :]
                low = c0 * prod[at, pl.ds(0, by)] - jnp.abs(c0) * prod[at, pl.ds(by, by)]
                high = c1 * prod[at, pl.ds(2 * by, by)] - jnp.abs(c1) * prod[at, pl.ds(3 * by, by)]
                tend[f, slab(k), :] = raw[f, k, pl.ds(LO, bx), :] - (high - low)
        return carry

    lax.fori_loop(0, nkg, along_y, 0)

    def along_x(k, fields):
        n = bx + 8
        c = raw[FU, k, pl.ds(LO, n), :] * scale
        wet = t0 <= k
        res = []
        for f in fields:
            sh = [raw[f, k, pl.ds(LO + o, n), :] for o in (-3, -2, -1, 0, 1, 2)]
            flux = stencil(c, *sh)
            nxt = pltpu.roll(flux, n - 1, 0)[:bx]
            res.append(jnp.where(wet, tend[f, slab(k), :] - (nxt - flux[:bx]), 0.0))
        return res

    def wait_ini(grp, c):
        for d in (WEST, EAST):
            wait_recv(d, *ini(d, grp, c))

    def first(k, acc):
        u, p = along_x(k, (FU, FP))
        p = HC * p
        u_out[k] = u
        pres[k, pl.ds(LO, bx), :] = p
        return jnp.where((lane >> 1) == k, pltpu.roll(p, 2 * k + 1, 1), acc)

    acc = zero
    for h in range(nh):
        for c in range(h * HALF // GROUP, (h + 1) * HALF // GROUP):
            wait_ini(0, c)
            acc = lax.fori_loop(c * GROUP, (c + 1) * GROUP, first, acc, unroll=4)
        start(WEST, uvx(h), stp(WEST, 0, h))
        start(EAST, stp(EAST, 0, h))
    ps_y[0] = acc
    start(SOUTH, stp(SOUTH, 0))
    start(NORTH, stp(NORTH, 0))

    def second(k, acc):
        v, w = along_x(k, (FV, FW))
        v_out[k] = v
        wsc[slab(k), :] = HC * w
        return jnp.where((lane >> 1) == k, pltpu.roll(v, 2 * k + 1, 1), acc)

    acc = zero
    for c in range(nkg):
        wait_ini(1, c)
        acc = lax.fori_loop(c * GROUP, (c + 1) * GROUP, second, acc, unroll=4)
    vs_y[...] = acc
    start(SOUTH, uvy())

    for d in (WEST, EAST):
        wait_send(d, *[x for grp in range(2) for c in range(nkg) for x in ini(d, grp, c)])
    for d in (SOUTH, NORTH):
        wait_send(d, *[iny(d, c) for c in range(nkg)])
    for d in (WEST, SOUTH):
        wait_send(d, ter(d))
    wait_send(WEST, *[uvx(h) for h in range(nh)])
    wait_send(SOUTH, uvy())
    wait_recv(WEST, *[uvx(h) for h in range(nh)])
    wait_recv(SOUTH, uvy())
    vh0 = pltpu.roll(vr_y[...], by - 1, 1)
    even = (lane & 1) == 0
    edge = jnp.logical_or(lane == 0, lane == by - 1)
    keep_w = jnp.broadcast_to(keep[0:1], (8, by))
    wet_lo = jnp.broadcast_to(t0[0:1], (8, by)) <= sub8
    wet_hi = jnp.broadcast_to(t0[bx - 1 : bx], (8, by)) <= sub8

    def inner(k0, n, masked):
        stores = []
        for i in range(n):
            k = k0 + i
            p0 = pres[k, pl.ds(LO, bx), :]
            pm = pres[k, pl.ds(LO - 1, bx), :]
            un = u_out[k] - (p0 - pm)
            vn = v_out[k] - (p0 - jnp.where(lane == 0, 0.0, pltpu.roll(p0, 1, 1)))
            if masked:
                wet = t0 <= k
                un = jnp.where(wet, un, 0.0)
                vn = jnp.where(wet, vn, 0.0)
            un1 = jnp.where(rows == bx - 1, 0.0, pltpu.roll(un, bx - 1, 0))
            vn1 = jnp.where(lane == by - 1, 0.0, pltpu.roll(vn, by - 1, 1))
            q = p0 - (g[k] * (HC * HC)) * ((un1 - un) + (vn1 - vn))
            ur = keep * un + relax * prof[0, k]
            vr = keep * vn + relax * prof[1, k]
            if masked:
                q = jnp.where(wet, q, 0.0)
                ur = jnp.where(wet, ur, 0.0)
                vr = jnp.where(wet, vr, 0.0)
            stores.append((k, q, ur, vr))
        for k, q, ur, vr in stores:
            q_buf[slab(k), :] = q
            u_out[k] = ur
            v_out[k] = vr

    def edges_y(k0, n, halo, masked):
        stores = []
        for i in range(n):
            k = k0 + i
            add = jnp.where(edge, pltpu.roll(halo, by - 1 - 2 * k, 1), 0.0)
            if masked:
                add = jnp.where(t0 <= k, add, 0.0)
            q = q_buf[slab(k), :] + (g[k] * (HC * HC)) * add
            v = v_out[k] + jnp.where(lane == 0, keep * add, 0.0)
            stores.append((k, q, v))
        for k, q, v in stores:
            q_buf[slab(k), :] = q
            v_out[k] = v

    wide = 8

    def over(body, *args):
        body(0, TERRAIN_MAX, *args, True)

        def step(n, carry):
            body(TERRAIN_MAX + n * wide, wide, *args, False)
            return carry

        lax.fori_loop(0, (nz - TERRAIN_MAX) // wide, step, 0)

    def substep(s, vh):
        over(inner)

        wait_recv(SOUTH, stp(SOUTH, s))
        wait_recv(NORTH, stp(NORTH, s))
        vn_h = wet_y * (vh - (pltpu.roll(pr_y[SOUTH - 2, s], by - 1, 1) - ps_y[s]))
        vh_next = vn_h - relax_hy * (vn_h - wet_y * vb_y)
        halo = jnp.where(even, -vn_h, pltpu.roll(pr_y[NORTH - 2, s], 1, 1))
        over(edges_y, halo)

        for d in (WEST, EAST):
            wait_recv(d, *[stp(d, s, h) for h in range(nh)])
        for n in range(0, nz, 8):
            at = pl.ds(n, 8)
            gh = gh_x[at, :]
            pw = pw_r[s, at, :]
            if n < TERRAIN_MAX:
                pw = jnp.where(wet_lo, pw, 0.0)
            first_row = pl.ds(n * bx, 8, stride=bx)
            last_row = pl.ds(n * bx + bx - 1, 8, stride=bx)
            q_buf[first_row, :] = q_buf[first_row, :] + gh * pw
            u_out[pl.ds(n, 8), 0, :] = u_out[pl.ds(n, 8), 0, :] + keep_w * pw
            wet = wet_x[at, :]
            un = wet * (uh_x[at, :] - (pe_r[s, at, :] - pres[pl.ds(n, 8), LO + bx - 1, :]))
            uh_x[at, :] = un - relax_hx * (un - wet * ub_x[at, :])
            if n < TERRAIN_MAX:
                un = jnp.where(wet_hi, un, 0.0)
            q_buf[last_row, :] = q_buf[last_row, :] - gh * un

        q_prev = q_buf[slab(0), :]
        x = zero
        for k in range(nz):
            at = slab(k)
            q = q_buf[slab(k + 1), :] if k < nz - 1 else zero
            x = wi[at, :] * (wsc[at, :] - ZC * (q - q_prev)) + li[at, :] * x
            if k < nz - 1:
                d_buf[at, :] = x
            q_prev = q

        for d in (WEST, EAST):
            wait_send(d, *[stp(d, s, h) for h in range(nh)])

        for h in range(nh - 1, -1, -1):
            for k in range((h + 1) * HALF - 1, h * HALF - 1, -1):
                below = zero
                if k > 0:
                    below = d_buf[slab(k - 1), :] + cc[slab(k - 1), :] * x
                pres[k, pl.ds(LO, bx), :] = (q_buf[slab(k), :] - (g[k] * ZC) * (x - below)) * keep
                wsc[slab(k), :] = x * keep
                x = below

            @pl.when(s < SUB - 1)
            def _(h=h):
                start(WEST, stp(WEST, s + 1, h))
                start(EAST, stp(EAST, s + 1, h))

        for d in (SOUTH, NORTH):
            wait_send(d, stp(d, s))

        @pl.when(s < SUB - 1)
        def _():
            acc = zero
            for k in range(nz):
                x = pltpu.roll(pres[k, pl.ds(LO, bx), :], 2 * k + 1, 1)
                acc = jnp.where((lane >> 1) == k, x, acc)
            ps_y[s + 1] = acc
            start(SOUTH, stp(SOUTH, s + 1))
            start(NORTH, stp(NORTH, s + 1))

        return vh_next

    lax.fori_loop(0, SUB, substep, vh0)

    def finish(k, carry):
        w_out[k] = wsc[slab(k), :] * (1.0 / HC)
        p_out[k] = pres[k, pl.ds(LO, bx), :] * (1.0 / HC)
        return carry

    lax.fori_loop(0, nz, finish, 0, unroll=4)


def solution(mesh):
    cnt = (mesh.shape["gx"], mesh.shape["gy"])

    def on_device(u, v, w, p, terr, zone, g, prof):
        nz, bx, by = u.shape
        assert by == 128 and bx == 16 and 2 * nz == by and nz % HALF == 0
        f32 = jnp.float32
        vm = pltpu.VMEM
        dma = pltpu.SemaphoreType.DMA
        nkg = nz // GROUP
        nh = nz // HALF
        lev = vm((nz * bx, by), f32)
        col = vm((nz, by), f32)
        plane = vm((bx, by), f32)
        scratch = [
            vm((4, nz, ROWS, by), f32),
            vm((4, nz * bx, by), f32),
            vm((nz, PEXT, by), f32),
            lev, lev, lev, lev, lev, lev,
            vm((GROUP * bx, 4 * by), jnp.bfloat16),
            vm((4 * by, 4 * by), jnp.bfloat16),
            vm((4 * by, by), jnp.bfloat16),
            vm((GROUP * bx, 4 * by), f32),
            vm((GROUP * bx, by), f32),
            vm((nkg, 4, bx, by), f32),
            vm((2, nkg, 4, bx, by), f32),
            vm((8, by), jnp.int32),
            vm((bx, by), jnp.int32),
            vm((SUB, nz, by), f32),
            vm((SUB, nz, by), f32),
            vm((SUB, bx, by), f32),
            vm((2, SUB, bx, by), f32),
            col, plane, plane, col, col, col,
            dma((4,)),
            dma((2, 2, nkg, 3)), dma((2, 2, nkg, 3)),
            dma((2, nkg)), dma((2, nkg)),
            dma((2,)), dma((2,)),
            dma((nh + 1,)), dma((nh + 1,)),
            dma((4, SUB, nh)), dma((4, SUB, nh)),
        ]
        vspec = pl.BlockSpec(memory_space=pltpu.VMEM)
        sspec = pl.BlockSpec(memory_space=pltpu.SMEM)
        aspec = pl.BlockSpec(memory_space=pl.ANY)
        return pl.pallas_call(
            functools.partial(kernel, nz, bx, cnt),
            out_shape=[pltpu.VMEM((nz, bx, by), f32)] * 4,
            in_specs=[aspec] * 4 + [vspec] + [sspec] * 3,
            out_specs=[vspec] * 4,
            scratch_shapes=scratch,
            compiler_params=pltpu.CompilerParams(collective_id=0, has_side_effects=True),
        )(u, v, w, p, terr, zone, g, prof)

    field = P(None, "gx", "gy")
    return jax.shard_map(
        on_device,
        mesh=mesh,
        in_specs=(field, field, field, field, P("gx", "gy"), P(), P(), P()),
        out_specs=(field,) * 4,
        check_vma=False,
    )
```

profile of v0, /device:TPU:0, one launch (start us, length us, event | category | flops | bytes accessed | tf_op | source)
XLA Modules:
  0.0 55.6 jit_solution(13142957167640463662)
XLA Ops:
  0.6 51.8 %shard_map.111 = (f32[64,16,128]{2,1,0:T(8,128)S(1)}, f32[64,16,128]{2,1,0:T(8,128)S(1)}, f32[64,16,128]{2,1,0:T(8,128)S(1)}, f32[64,16,128]{2,1,0:T(8,128)S(1)}) custom-call(f32[64,16,128]{2,1,0:T(8,128)} %u_in.1, f32[64,16,128]{2,1,0:T(8,128)} %v_in.1, f32[64,16,128]{2,1,0:T(8,128)} %w_in.1, f32[64,16,128]{2,1,0:T(8,128)} %p_in.1, s32[16,128]{1,0:T(8,128)} %terr.1, ...), custom_call_target="tpu_custom_call" | custom-call | tf_op jit(solution)/shard_map/pallas_call | solution.py:600
  52.4 0.8 %copy.16 = f32[64,16,128]{2,1,0:T(8,128)} copy(f32[64,16,128]{2,1,0:T(8,128)S(1)} %get-tuple-element.4) | data formatting | bytes 1048576
  53.2 0.8 %copy.17 = f32[64,16,128]{2,1,0:T(8,128)} copy(f32[64,16,128]{2,1,0:T(8,128)S(1)} %get-tuple-element.5) | data formatting | bytes 1048576
  54.0 0.8 %copy.18 = f32[64,16,128]{2,1,0:T(8,128)} copy(f32[64,16,128]{2,1,0:T(8,128)S(1)} %get-tuple-element.6) | data formatting | bytes 1048576
  54.8 0.8 %copy.19 = f32[64,16,128]{2,1,0:T(8,128)} copy(f32[64,16,128]{2,1,0:T(8,128)S(1)} %get-tuple-element.7) | data formatting | bytes 1048576
where the time goes:
time: 55.8 us; the launch traced here: 55.6 us
  Pallas kernels  51.8 us (93%)
  local copies, waits for them, and re-layouts  3.17 us (6%)
  between operations  0.64 us (1%)
    pallas_call x1, Pallas kernels, on_device(): pl.pallas_call(functools.partial(kernel, nz, bx, cnt), out_shape=[pltpu.V...  51.8 us
    unnamed x4, local copies, waits for them, and re-layouts  3.17 us

commit v1 on v0

--- a/solution.py
+++ b/solution.py
@@ -51,14 +51,18 @@
     v_in,
     w_in,
     p_in,
+    terr_in,
+    zone_in,
+    g_in,
+    prof_in,
+    u_out,
+    v_out,
+    w_out,
+    p_out,
     terr,
     zone,
     g,
     prof,
-    u_out,
-    v_out,
-    w_out,
-    p_out,
     raw,
     tend,
     pres,
@@ -98,6 +102,10 @@
     uv_r,
     stp_s,
     stp_r,
+    hop,
+    hop_s,
+    hop_r,
+    fwd_s,
 ):
     by = 128
     nkg = nz // GROUP
@@ -109,21 +117,35 @@
     peer = ({"gx": gx - 1}, {"gx": gx + 1}, {"gy": gy - 1}, {"gy": gy + 1})
     opp = (EAST, WEST, NORTH, SOUTH)
 
+    relay = nx_dev == 4
+    inner_x = jnp.logical_or(gx == 1, gx == 2)
+
+    barrier = pltpu.get_barrier_semaphore()
+
+    def greet(dev):
+        pl.semaphore_signal(barrier, inc=1, device_id=dev, device_id_type=pl.DeviceIdType.MESH)
+
+    for d in range(4):
+
+        @pl.when(has[d])
+        def _(d=d):
+            greet(peer[d])
+
+    if relay:
+        greet({"gx": lax.rem(gx + 2, 4)})
+
     loads = [
         pltpu.make_async_copy(src, raw.at[f, :, pl.ds(LO, bx), :], in_s.at[f])
         for f, src in ((FU, u_in), (FP, p_in), (FV, v_in), (FW, w_in))
     ]
-    for c in loads:
+    small = [
+        pltpu.make_async_copy(src, dst, in_s.at[4 + n])
+        for n, (src, dst) in enumerate(
+            ((terr_in, terr), (zone_in, zone), (g_in, g), (prof_in, prof))
+        )
+    ]
+    for c in loads + small:
         c.start()
-
-    barrier = pltpu.get_barrier_semaphore()
-    for d in range(4):
-
-        @pl.when(has[d])
-        def _(d=d):
-            pl.semaphore_signal(
-                barrier, inc=1, device_id=peer[d], device_id_type=pl.DeviceIdType.MESH
-            )
 
     def rcopy(d, src, dst, ss, rs):
         return pltpu.make_async_remote_copy(
@@ -170,6 +192,32 @@
             )
         return out
 
+    def direct(d):
+        if not relay:
+            return has[d]
+        return jnp.logical_and(has[d], gx != (2, 1)[d])
+
+    def rcopy_to(dev, src, dst, ss, rs):
+        return pltpu.make_async_remote_copy(
+            src_ref=src,
+            dst_ref=dst,
+            send_sem=ss,
+            recv_sem=rs,
+            device_id={"gx": dev},
+            device_id_type=pl.DeviceIdType.MESH,
+        )
+
+    def to_relay(d, c):
+        return [
+            (x[0], hop.at[c, r], hop_s.at[c, r], hop_r.at[c, r])
+            for r, x in enumerate(ini(d, 1, c))
+        ]
+
+    def from_relay(d, c):
+        return [
+            (hop.at[c, r], x[1], fwd_s.at[c, r], x[3]) for r, x in enumerate(ini(d, 1, c))
+        ]
+
     def iny(d, c):
         return ys.at[c], yr.at[d - 2, c], iny_s.at[d - 2, c], iny_r.at[d - 2, c]
 
@@ -234,17 +282,35 @@
                 tr_y[...] = jnp.full(tr_y.shape, DRY, jnp.int32)
                 vr_y[...] = jnp.zeros(vr_y.shape, jnp.float32)
 
+    small[0].wait()
     loads[0].wait()
     loads[1].wait()
-    pl.semaphore_wait(barrier, sum(h.astype(jnp.int32) for h in has))
+    pl.semaphore_wait(barrier, sum(h.astype(jnp.int32) for h in has) + int(relay))
+    start(WEST, ter(WEST))
+    start(SOUTH, ter(SOUTH))
     start(WEST, *[x for c in range(nkg) for x in ini(WEST, 0, c)])
     start(EAST, *[x for c in range(nkg) for x in ini(EAST, 0, c)])
-    start(WEST, ter(WEST))
-    start(SOUTH, ter(SOUTH))
     loads[2].wait()
     loads[3].wait()
-    start(WEST, *[x for c in range(nkg) for x in ini(WEST, 1, c)])
-    start(EAST, *[x for c in range(nkg) for x in ini(EAST, 1, c)])
+    if relay:
+        for d, at in ((EAST, 1), (WEST, 2)):
+
+            @pl.when(gx == at)
+            def _(d=d):
+                for c in range(nkg):
+                    for x in to_relay(d, c):
+                        rcopy_to(lax.rem(gx + 2, 4), *x).start()
+
+    for d in (WEST, EAST):
+
+        @pl.when(direct(d))
+        def _(d=d):
+            for c in range(nkg):
+                for x in ini(d, 1, c):
+                    rcopy(d, *x).start()
+
+    for c in small[1:]:
+        c.wait()
 
     def pack(kg, carry):
         for f in range(4):
@@ -312,15 +378,7 @@
 
     _, vb_y = lax.fori_loop(0, nz, coeff, (zero, zero))
 
-    wait_recv(WEST, ter(WEST))
-    wait_recv(SOUTH, ter(SOUTH))
     sub8 = lax.broadcasted_iota(jnp.int32, (8, by), 0)
-    t_east = jnp.broadcast_to(trx[0:1, :], (8, by))
-    for k in range(0, nz, 8):
-        wet_x[pl.ds(k, 8), :] = jnp.where(t_east <= sub8 + k, 1.0, 0.0)
-    t_north = jnp.broadcast_to(tr_y[:, 0:1], (bx, by))
-    wet_y = jnp.where(t_north <= (lane >> 1), 1.0, 0.0)
-
     scale = ADV / 60.0
 
     def along_y(kg, carry):
@@ -357,6 +415,25 @@
 
     lax.fori_loop(0, nkg, along_y, 0)
 
+    if relay:
+        for d, at in ((EAST, 3), (WEST, 0)):
+
+            @pl.when(gx == at)
+            def _(d=d):
+                for c in range(nkg):
+                    for x, y in zip(to_relay(d, c), from_relay(d, c)):
+                        rcopy_to(lax.rem(gx + 2, 4), *x).wait_recv()
+                        rcopy_to((gx + 1, gx - 1)[d == EAST], *y).start()
+
+    wait_recv(WEST, ter(WEST))
+    wait_recv(SOUTH, ter(SOUTH))
+    t_east = jnp.broadcast_to(trx[0:1, :], (8, by))
+    for k in range(0, nz, 8):
+        wet_x[pl.ds(k, 8), :] = jnp.where(t_east <= sub8 + k, 1.0, 0.0)
+    t_north = jnp.broadcast_to(tr_y[:, 0:1], (bx, by))
+    wet_y = jnp.where(t_north <= (lane >> 1), 1.0, 0.0)
+
+
     def along_x(k, fields):
         n = bx + 8
         c = raw[FU, k, pl.ds(LO, n), :] * scale
@@ -405,7 +482,28 @@
     start(SOUTH, uvy())
 
     for d in (WEST, EAST):
-        wait_send(d, *[x for grp in range(2) for c in range(nkg) for x in ini(d, grp, c)])
+        wait_send(d, *[x for c in range(nkg) for x in ini(d, 0, c)])
+
+        @pl.when(direct(d))
+        def _(d=d):
+            for c in range(nkg):
+                for x in ini(d, 1, c):
+                    rcopy(d, *x).wait_send()
+
+    if relay:
+
+        @pl.when(inner_x)
+        def _():
+            for c in range(nkg):
+                for x in to_relay(EAST, c):
+                    rcopy_to(lax.rem(gx + 2, 4), *x).wait_send()
+
+        @pl.when(jnp.logical_not(inner_x))
+        def _():
+            for c in range(nkg):
+                for x in from_relay(EAST, c):
+                    rcopy_to(lax.rem(gx + 2, 4), *x).wait_send()
+
     for d in (SOUTH, NORTH):
         wait_send(d, *[iny(d, c) for c in range(nkg)])
     for d in (WEST, SOUTH):
@@ -568,7 +666,12 @@
         lev = vm((nz * bx, by), f32)
         col = vm((nz, by), f32)
         plane = vm((bx, by), f32)
+        plane_i = vm((bx, by), jnp.int32)
         scratch = [
+            plane_i,
+            pltpu.SMEM(zone.shape, jnp.int32),
+            pltpu.SMEM(g.shape, f32),
+            pltpu.SMEM(prof.shape, f32),
             vm((4, nz, ROWS, by), f32),
             vm((4, nz * bx, by), f32),
             vm((nz, PEXT, by), f32),
@@ -587,20 +690,21 @@
             vm((SUB, bx, by), f32),
             vm((2, SUB, bx, by), f32),
             col, plane, plane, col, col, col,
-            dma((4,)),
+            dma((8,)),
             dma((2, 2, nkg, 3)), dma((2, 2, nkg, 3)),
             dma((2, nkg)), dma((2, nkg)),
             dma((2,)), dma((2,)),
             dma((nh + 1,)), dma((nh + 1,)),
             dma((4, SUB, nh)), dma((4, SUB, nh)),
+            vm((nkg, 3, 2, GROUP, by), f32),
+            dma((nkg, 3)), dma((nkg, 3)), dma((nkg, 3)),
         ]
         vspec = pl.BlockSpec(memory_space=pltpu.VMEM)
-        sspec = pl.BlockSpec(memory_space=pltpu.SMEM)
         aspec = pl.BlockSpec(memory_space=pl.ANY)
         return pl.pallas_call(
             functools.partial(kernel, nz, bx, cnt),
             out_shape=[pltpu.VMEM((nz, bx, by), f32)] * 4,
-            in_specs=[aspec] * 4 + [vspec] + [sspec] * 3,
+            in_specs=[aspec] * 8,
             out_specs=[vspec] * 4,
             scratch_shapes=scratch,
             compiler_params=pltpu.CompilerParams(collective_id=0, has_side_effects=True),

time: 55.8 us -> 51 us (0.914)
  Pallas kernels: 51.8 us -> 47.1 us
    pallas_call x1, Pallas kernels: 51.8 us -> 47.1 us  [on_device(): pl.pallas_call(functools.partial(kernel, nz, bx, cnt), out_shape=[pltpu.V...]
where the time goes in v1:
time: 51 us; the launch traced here: 50.9 us
  Pallas kernels  47.1 us (92%)
  local copies, waits for them, and re-layouts  3.17 us (6%)
  between operations  0.64 us (1%)
    pallas_call x1, Pallas kernels, on_device(): pl.pallas_call(functools.partial(kernel, nz, bx, cnt), out_shape=[pltpu.V...  47.1 us
    unnamed x4, local copies, waits for them, and re-layouts  3.17 us

profile of v1, /device:TPU:0, one launch (start us, length us, event | category | flops | bytes accessed | tf_op | source)
XLA Modules:
  0.0 50.9 jit_solution(4216570601625467508)
XLA Ops:
  0.6 47.1 %shard_map.111 = (f32[64,16,128]{2,1,0:T(8,128)S(1)}, f32[64,16,128]{2,1,0:T(8,128)S(1)}, f32[64,16,128]{2,1,0:T(8,128)S(1)}, f32[64,16,128]{2,1,0:T(8,128)S(1)}) custom-call(f32[64,16,128]{2,1,0:T(8,128)} %u_in.1, f32[64,16,128]{2,1,0:T(8,128)} %v_in.1, f32[64,16,128]{2,1,0:T(8,128)} %w_in.1, f32[64,16,128]{2,1,0:T(8,128)} %p_in.1, s32[16,128]{1,0:T(8,128)} %terr_in.1, ...), custom_call_target="tpu_custom_call" | custom-call | tf_op jit(solution)/shard_map/pallas_call | solution.py:704
  47.7 0.8 %copy.16 = f32[64,16,128]{2,1,0:T(8,128)} copy(f32[64,16,128]{2,1,0:T(8,128)S(1)} %get-tuple-element.4) | data formatting | bytes 1048576
  48.5 0.8 %copy.17 = f32[64,16,128]{2,1,0:T(8,128)} copy(f32[64,16,128]{2,1,0:T(8,128)S(1)} %get-tuple-element.5) | data formatting | bytes 1048576
  49.3 0.8 %copy.18 = f32[64,16,128]{2,1,0:T(8,128)} copy(f32[64,16,128]{2,1,0:T(8,128)S(1)} %get-tuple-element.6) | data formatting | bytes 1048576
  50.1 0.8 %copy.19 = f32[64,16,128]{2,1,0:T(8,128)} copy(f32[64,16,128]{2,1,0:T(8,128)S(1)} %get-tuple-element.7) | data formatting | bytes 1048576

commit v2 on v1

--- a/solution.py
+++ b/solution.py
@@ -20,7 +20,6 @@
 ROWS = 40
 PEXT = 32
 GROUP = 16
-HALF = 32
 CENT = {-3: 1.0, -2: -8.0, -1: 37.0, 0: 37.0, 1: -8.0, 2: 1.0}
 UPW = {-3: -1.0, -2: 5.0, -1: -10.0, 0: 10.0, 1: -5.0, 2: 1.0}
 
@@ -85,6 +84,7 @@
     pe_r,
     ps_y,
     pr_y,
+    us_x,
     uh_x,
     vs_y,
     vr_y,
@@ -109,7 +109,6 @@
 ):
     by = 128
     nkg = nz // GROUP
-    nh = nz // HALF
     gx = lax.axis_index("gx")
     gy = lax.axis_index("gy")
     nx_dev, ny_dev = cnt
@@ -175,22 +174,17 @@
             for c in copies:
                 rcopy(d, *c).wait_recv()
 
-    def ini(d, grp, c):
-        out = []
-        for r in range(3):
-            own = LO + r if d == WEST else LO + bx - 3 + r
-            far = LO + bx + r if d == WEST else LO - 3 + r
-            f = pl.ds(2 * grp, 2)
-            k = pl.ds(c * GROUP, GROUP)
-            out.append(
-                (
-                    raw.at[f, k, own, :],
-                    raw.at[f, k, far, :],
-                    ini_s.at[d, grp, c, r],
-                    ini_r.at[d, grp, c, r],
-                )
-            )
-        return out
+    def ini(d, grp, c=None):
+        own = LO if d == WEST else LO + bx - 3
+        far = LO + bx if d == WEST else LO - 3
+        f = pl.ds(0, 2) if grp == 0 else grp + 1
+        k = pl.ds(0, nz) if c is None else pl.ds(c * GROUP, GROUP)
+        return (
+            raw.at[f, k, pl.ds(own, 3), :],
+            raw.at[f, k, pl.ds(far, 3), :],
+            ini_s.at[d, grp],
+            ini_r.at[d, grp, 0 if c is None else c],
+        )
 
     def direct(d):
         if not relay:
@@ -207,38 +201,51 @@
             device_id_type=pl.DeviceIdType.MESH,
         )
 
-    def to_relay(d, c):
-        return [
-            (x[0], hop.at[c, r], hop_s.at[c, r], hop_r.at[c, r])
-            for r, x in enumerate(ini(d, 1, c))
-        ]
-
-    def from_relay(d, c):
-        return [
-            (hop.at[c, r], x[1], fwd_s.at[c, r], x[3]) for r, x in enumerate(ini(d, 1, c))
-        ]
+    def to_relay(d, grp):
+        dst = hop.at[grp - 1, :, pl.ds(0, 3), :]
+        return ini(d, grp)[0], dst, hop_s.at[grp - 1], hop_r.at[grp - 1]
+
+    def from_relay(d, grp, c=None):
+        k = pl.ds(0, nz) if c is None else pl.ds(c * GROUP, GROUP)
+        _, dst, _, sem = ini(d, grp, c)
+        return hop.at[grp - 1, k, pl.ds(0, 3), :], dst, fwd_s.at[grp - 1], sem
+
+    def forward(grp):
+        if relay:
+            for d, at in ((EAST, 3), (WEST, 0)):
+
+                @pl.when(gx == at)
+                def _(d=d):
+                    rcopy_to(lax.rem(gx + 2, 4), *to_relay(d, grp)).wait_recv()
+                    for c in range(nkg):
+                        rcopy_to((gx + 1, gx - 1)[d == EAST], *from_relay(d, grp, c)).start()
+
+    def start_direct(grp):
+        for d in (WEST, EAST):
+
+            @pl.when(direct(d))
+            def _(d=d):
+                for c in range(nkg):
+                    rcopy(d, *ini(d, grp, c)).start()
 
     def iny(d, c):
-        return ys.at[c], yr.at[d - 2, c], iny_s.at[d - 2, c], iny_r.at[d - 2, c]
+        return ys.at[c], yr.at[d - 2, c], iny_s.at[d - 2], iny_r.at[d - 2, c]
 
     def ter(d):
         if d == WEST:
             return terr.at[pl.ds(0, 8)], trx, ter_s.at[0], ter_r.at[0]
         return terr, tr_y, ter_s.at[1], ter_r.at[1]
 
-    def uvx(h):
-        k = pl.ds(h * HALF, HALF)
-        return u_out.at[k, 0, :], uh_x.at[k], uv_s.at[h], uv_r.at[h]
-
-    def uvy():
-        return vs_y, vr_y, uv_s.at[nh], uv_r.at[nh]
-
-    def stp(d, s, h=0):
-        sems = stp_s.at[d, s, h], stp_r.at[d, s, h]
+    def uv(d):
+        if d == WEST:
+            return us_x, uh_x, uv_s.at[0], uv_r.at[0]
+        return vs_y, vr_y, uv_s.at[1], uv_r.at[1]
+
+    def stp(d, s):
+        sems = stp_s.at[d], stp_r.at[d, lax.rem(s, 2)]
         if d < 2:
-            k = pl.ds(h * HALF, HALF)
             row = LO if d == WEST else LO + bx - 1
-            return pres.at[k, row, :], (pe_r, pw_r)[d].at[s, k], *sems
+            return pres.at[:, row, :], (pe_r, pw_r)[d].at[s], *sems
         return ps_y.at[s], pr_y.at[d - 2, s], *sems
 
     rows = lax.broadcasted_iota(jnp.int32, (bx, by), 0)
@@ -288,8 +295,8 @@
     pl.semaphore_wait(barrier, sum(h.astype(jnp.int32) for h in has) + int(relay))
     start(WEST, ter(WEST))
     start(SOUTH, ter(SOUTH))
-    start(WEST, *[x for c in range(nkg) for x in ini(WEST, 0, c)])
-    start(EAST, *[x for c in range(nkg) for x in ini(EAST, 0, c)])
+    for d in (WEST, EAST):
+        start(d, *[ini(d, 0, c) for c in range(nkg)])
     loads[2].wait()
     loads[3].wait()
     if relay:
@@ -297,17 +304,10 @@
 
             @pl.when(gx == at)
             def _(d=d):
-                for c in range(nkg):
-                    for x in to_relay(d, c):
-                        rcopy_to(lax.rem(gx + 2, 4), *x).start()
-
-    for d in (WEST, EAST):
-
-        @pl.when(direct(d))
-        def _(d=d):
-            for c in range(nkg):
-                for x in ini(d, 1, c):
-                    rcopy(d, *x).start()
+                for grp in (1, 2):
+                    rcopy_to(lax.rem(gx + 2, 4), *to_relay(d, grp)).start()
+
+    start_direct(1)
 
     for c in small[1:]:
         c.wait()
@@ -415,15 +415,8 @@
 
     lax.fori_loop(0, nkg, along_y, 0)
 
-    if relay:
-        for d, at in ((EAST, 3), (WEST, 0)):
-
-            @pl.when(gx == at)
-            def _(d=d):
-                for c in range(nkg):
-                    for x, y in zip(to_relay(d, c), from_relay(d, c)):
-                        rcopy_to(lax.rem(gx + 2, 4), *x).wait_recv()
-                        rcopy_to((gx + 1, gx - 1)[d == EAST], *y).start()
+    forward(1)
+    start_direct(2)
 
     wait_recv(WEST, ter(WEST))
     wait_recv(SOUTH, ter(SOUTH))
@@ -448,7 +441,7 @@
 
     def wait_ini(grp, c):
         for d in (WEST, EAST):
-            wait_recv(d, *ini(d, grp, c))
+            wait_recv(d, ini(d, grp, c))
 
     def first(k, acc):
         u, p = along_x(k, (FU, FP))
@@ -458,66 +451,18 @@
         return jnp.where((lane >> 1) == k, pltpu.roll(p, 2 * k + 1, 1), acc)
 
     acc = zero
-    for h in range(nh):
-        for c in range(h * HALF // GROUP, (h + 1) * HALF // GROUP):
-            wait_ini(0, c)
-            acc = lax.fori_loop(c * GROUP, (c + 1) * GROUP, first, acc, unroll=4)
-        start(WEST, uvx(h), stp(WEST, 0, h))
-        start(EAST, stp(EAST, 0, h))
+    for c in range(nkg):
+        wait_ini(0, c)
+        acc = lax.fori_loop(c * GROUP, (c + 1) * GROUP, first, acc, unroll=4)
+    for n in range(0, nz, 8):
+        us_x[pl.ds(n, 8), :] = u_out[pl.ds(n, 8), 0, :]
+    start(WEST, stp(WEST, 0), uv(WEST))
+    start(EAST, stp(EAST, 0))
     ps_y[0] = acc
     start(SOUTH, stp(SOUTH, 0))
     start(NORTH, stp(NORTH, 0))
 
-    def second(k, acc):
-        v, w = along_x(k, (FV, FW))
-        v_out[k] = v
-        wsc[slab(k), :] = HC * w
-        return jnp.where((lane >> 1) == k, pltpu.roll(v, 2 * k + 1, 1), acc)
-
-    acc = zero
-    for c in range(nkg):
-        wait_ini(1, c)
-        acc = lax.fori_loop(c * GROUP, (c + 1) * GROUP, second, acc, unroll=4)
-    vs_y[...] = acc
-    start(SOUTH, uvy())
-
-    for d in (WEST, EAST):
-        wait_send(d, *[x for c in range(nkg) for x in ini(d, 0, c)])
-
-        @pl.when(direct(d))
-        def _(d=d):
-            for c in range(nkg):
-                for x in ini(d, 1, c):
-                    rcopy(d, *x).wait_send()
-
-    if relay:
-
-        @pl.when(inner_x)
-        def _():
-            for c in range(nkg):
-                for x in to_relay(EAST, c):
-                    rcopy_to(lax.rem(gx + 2, 4), *x).wait_send()
-
-        @pl.when(jnp.logical_not(inner_x))
-        def _():
-            for c in range(nkg):
-                for x in from_relay(EAST, c):
-                    rcopy_to(lax.rem(gx + 2, 4), *x).wait_send()
-
-    for d in (SOUTH, NORTH):
-        wait_send(d, *[iny(d, c) for c in range(nkg)])
-    for d in (WEST, SOUTH):
-        wait_send(d, ter(d))
-    wait_send(WEST, *[uvx(h) for h in range(nh)])
-    wait_send(SOUTH, uvy())
-    wait_recv(WEST, *[uvx(h) for h in range(nh)])
-    wait_recv(SOUTH, uvy())
-    vh0 = pltpu.roll(vr_y[...], by - 1, 1)
-    even = (lane & 1) == 0
-    edge = jnp.logical_or(lane == 0, lane == by - 1)
-    keep_w = jnp.broadcast_to(keep[0:1], (8, by))
-    wet_lo = jnp.broadcast_to(t0[0:1], (8, by)) <= sub8
-    wet_hi = jnp.broadcast_to(t0[bx - 1 : bx], (8, by)) <= sub8
+    forward(2)
 
     def inner(k0, n, masked):
         stores = []
@@ -546,19 +491,47 @@
             u_out[k] = ur
             v_out[k] = vr
 
-    def edges_y(k0, n, halo, masked):
-        stores = []
-        for i in range(n):
-            k = k0 + i
+    def second(k, acc):
+        (v,) = along_x(k, (FV,))
+        v_out[k] = v
+        return jnp.where((lane >> 1) == k, pltpu.roll(v, 2 * k + 1, 1), acc)
+
+    def third(k, carry):
+        wsc[slab(k), :] = HC * along_x(k, (FW,))[0]
+        return carry
+
+    acc = zero
+    for c in range(nkg):
+        wait_ini(1, c)
+        acc = lax.fori_loop(c * GROUP, (c + 1) * GROUP, second, acc, unroll=4)
+        if c == 0:
+            inner(0, TERRAIN_MAX, True)
+            inner(TERRAIN_MAX, GROUP - TERRAIN_MAX, False)
+        else:
+            inner(c * GROUP, GROUP, False)
+    vs_y[...] = acc
+    start(SOUTH, uv(SOUTH))
+
+    for c in range(nkg):
+        wait_ini(2, c)
+        lax.fori_loop(c * GROUP, (c + 1) * GROUP, third, 0, unroll=4)
+
+    wait_recv(WEST, uv(WEST))
+    wait_recv(SOUTH, uv(SOUTH))
+    vh0 = pltpu.roll(vr_y[...], by - 1, 1)
+    even = (lane & 1) == 0
+    edge = jnp.logical_or(lane == 0, lane == by - 1)
+    keep_w = jnp.broadcast_to(keep[0:1], (8, by))
+    wet_lo = jnp.broadcast_to(t0[0:1], (8, by)) <= sub8
+    wet_hi = jnp.broadcast_to(t0[bx - 1 : bx], (8, by)) <= sub8
+
+    def edges_y(halo):
+        for k in range(nz):
             add = jnp.where(edge, pltpu.roll(halo, by - 1 - 2 * k, 1), 0.0)
-            if masked:
+            if k < TERRAIN_MAX:
                 add = jnp.where(t0 <= k, add, 0.0)
-            q = q_buf[slab(k), :] + (g[k] * (HC * HC)) * add
-            v = v_out[k] + jnp.where(lane == 0, keep * add, 0.0)
-            stores.append((k, q, v))
-        for k, q, v in stores:
-            q_buf[slab(k), :] = q
-            v_out[k] = v
+            q_buf[slab(k), :] = q_buf[slab(k), :] + (g[k] * (HC * HC)) * add
+            v_out[k] = v_out[k] + jnp.where(lane == 0, keep * add, 0.0)
 
     wide = 8
 
@@ -572,17 +545,15 @@
         lax.fori_loop(0, (nz - TERRAIN_MAX) // wide, step, 0)
 
     def substep(s, vh):
-        over(inner)
-
         wait_recv(SOUTH, stp(SOUTH, s))
         wait_recv(NORTH, stp(NORTH, s))
         vn_h = wet_y * (vh - (pltpu.roll(pr_y[SOUTH - 2, s], by - 1, 1) - ps_y[s]))
         vh_next = vn_h - relax_hy * (vn_h - wet_y * vb_y)
         halo = jnp.where(even, -vn_h, pltpu.roll(pr_y[NORTH - 2, s], 1, 1))
-        over(edges_y, halo)
+        edges_y(halo)
 
         for d in (WEST, EAST):
-            wait_recv(d, *[stp(d, s, h) for h in range(nh)])
+            wait_recv(d, stp(d, s))
         for n in range(0, nz, 8):
             at = pl.ds(n, 8)
             gh = gh_x[at, :]
@@ -611,21 +582,20 @@
             q_prev = q
 
         for d in (WEST, EAST):
-            wait_send(d, *[stp(d, s, h) for h in range(nh)])
-
-        for h in range(nh - 1, -1, -1):
-            for k in range((h + 1) * HALF - 1, h * HALF - 1, -1):
-                below = zero
-                if k > 0:
-                    below = d_buf[slab(k - 1), :] + cc[slab(k - 1), :] * x
-                pres[k, pl.ds(LO, bx), :] = (q_buf[slab(k), :] - (g[k] * ZC) * (x - below)) * keep
-                wsc[slab(k), :] = x * keep
-                x = below
-
-            @pl.when(s < SUB - 1)
-            def _(h=h):
-                start(WEST, stp(WEST, s + 1, h))
-                start(EAST, stp(EAST, s + 1, h))
+            wait_send(d, stp(d, s))
+
+        for k in range(nz - 1, -1, -1):
+            below = zero
+            if k > 0:
+                below = d_buf[slab(k - 1), :] + cc[slab(k - 1), :] * x
+            pres[k, pl.ds(LO, bx), :] = (q_buf[slab(k), :] - (g[k] * ZC) * (x - below)) * keep
+            wsc[slab(k), :] = x * keep
+            x = below
+
+        @pl.when(s < SUB - 1)
+        def _():
+            start(WEST, stp(WEST, s + 1))
+            start(EAST, stp(EAST, s + 1))
 
         for d in (SOUTH, NORTH):
             wait_send(d, stp(d, s))
@@ -639,10 +609,36 @@
             ps_y[s + 1] = acc
             start(SOUTH, stp(SOUTH, s + 1))
             start(NORTH, stp(NORTH, s + 1))
+            over(inner)
 
         return vh_next
 
     lax.fori_loop(0, SUB, substep, vh0)
+
+    for d in (WEST, EAST):
+        wait_send(d, ini(d, 0))
+
+        @pl.when(direct(d))
+        def _(d=d):
+            for grp in (1, 2):
+                rcopy(d, *ini(d, grp)).wait_send()
+
+    if relay:
+
+        @pl.when(inner_x)
+        def _():
+            for grp in (1, 2):
+                rcopy_to(lax.rem(gx + 2, 4), *to_relay(EAST, grp)).wait_send()
+
+        @pl.when(jnp.logical_not(inner_x))
+        def _():
+            for grp in (1, 2):
+                rcopy_to(lax.rem(gx + 2, 4), *from_relay(EAST, grp)).wait_send()
+
+    for d in (SOUTH, NORTH):
+        wait_send(d, (ys, yr.at[d - 2], iny_s.at[d - 2], iny_r.at[d - 2, 0]))
+    for d in (WEST, SOUTH):
+        wait_send(d, ter(d), uv(d))
 
     def finish(k, carry):
         w_out[k] = wsc[slab(k), :] * (1.0 / HC)
@@ -652,17 +648,25 @@
     lax.fori_loop(0, nz, finish, 0, unroll=4)
 
 
+def emit(*refs):
+    sems = refs[-1]
+    copies = [pltpu.make_async_copy(refs[n], refs[4 + n], sems.at[n]) for n in range(4)]
+    for c in copies:
+        c.start()
+    for c in copies:
+        c.wait()
+
+
 def solution(mesh):
     cnt = (mesh.shape["gx"], mesh.shape["gy"])
 
     def on_device(u, v, w, p, terr, zone, g, prof):
         nz, bx, by = u.shape
-        assert by == 128 and bx == 16 and 2 * nz == by and nz % HALF == 0
+        assert by == 128 and bx == 16 and 2 * nz == by
         f32 = jnp.float32
         vm = pltpu.VMEM
         dma = pltpu.SemaphoreType.DMA
         nkg = nz // GROUP
-        nh = nz // HALF
         lev = vm((nz * bx, by), f32)
         col = vm((nz, by), f32)
         plane = vm((bx, by), f32)
@@ -689,19 +693,19 @@
             vm((SUB, nz, by), f32),
             vm((SUB, bx, by), f32),
             vm((2, SUB, bx, by), f32),
-            col, plane, plane, col, col, col,
+            col, col, plane, plane, col, col, col,
             dma((8,)),
-            dma((2, 2, nkg, 3)), dma((2, 2, nkg, 3)),
-            dma((2, nkg)), dma((2, nkg)),
+            dma((2, 3)), dma((2, 3, nkg)),
+            dma((2,)), dma((2, nkg)),
             dma((2,)), dma((2,)),
-            dma((nh + 1,)), dma((nh + 1,)),
-            dma((4, SUB, nh)), dma((4, SUB, nh)),
-            vm((nkg, 3, 2, GROUP, by), f32),
-            dma((nkg, 3)), dma((nkg, 3)), dma((nkg, 3)),
+            dma((2,)), dma((2,)),
+            dma((4,)), dma((4, 2)),
+            vm((2, nz, 8, by), f32),
+            dma((2,)), dma((2,)), dma((2,)),
         ]
         vspec = pl.BlockSpec(memory_space=pltpu.VMEM)
         aspec = pl.BlockSpec(memory_space=pl.ANY)
-        return pl.pallas_call(
+        outs = pl.pallas_call(
             functools.partial(kernel, nz, bx, cnt),
             out_shape=[pltpu.VMEM((nz, bx, by), f32)] * 4,
             in_specs=[aspec] * 8,
@@ -709,6 +713,14 @@
             scratch_shapes=scratch,
             compiler_params=pltpu.CompilerParams(collective_id=0, has_side_effects=True),
         )(u, v, w, p, terr, zone, g, prof)
+        outs = [pltpu.with_memory_space_constraint(a, pltpu.VMEM) for a in outs]
+        return pl.pallas_call(
+            emit,
+            out_shape=[jax.ShapeDtypeStruct((nz, bx, by), f32)] * 4,
+            in_specs=[vspec] * 4,
+            out_specs=[aspec] * 4,
+            scratch_shapes=[dma((4,))],
+        )(*outs)
 
     field = P(None, "gx", "gy")
     return jax.shard_map(

time: 51 us -> 43.8 us (0.86)
  Pallas kernels: 47.1 us -> 43 us
  local copies, waits for them, and re-layouts: 3.17 us -> 0 us
    pallas_call x1, Pallas kernels: 47.1 us -> 41.6 us  [on_device(): pl.pallas_call(functools.partial(kernel, nz, bx, cnt), out_shape=[pltpu.V...]
    unnamed x4 -> x0, local copies, waits for them, and re-layouts: 3.17 us -> none
    pallas_call x0 -> x1, Pallas kernels: none -> 1.35 us  [on_device(): pl.pallas_call(emit, out_shape=[jax.ShapeDtypeStruct((nz, bx, by), f32)]...]
where the time goes in v2:
time: 43.8 us; the launch traced here: 43.6 us
  Pallas kernels  43 us (98%)
  between operations  0.64 us (1%)
    pallas_call x1, Pallas kernels, on_device(): pl.pallas_call(functools.partial(kernel, nz, bx, cnt), out_shape=[pltpu.V...  41.6 us
    pallas_call x1, Pallas kernels, on_device(): pl.pallas_call(emit, out_shape=[jax.ShapeDtypeStruct((nz, bx, by), f32)]...  1.35 us

profile of v2, /device:TPU:0, one launch (start us, length us, event | category | flops | bytes accessed | tf_op | source)
XLA Modules:
  0.0 43.6 jit_solution(17089263130993561249)
XLA Ops:
  0.6 41.6 %shard_map.111 = (f32[64,16,128]{2,1,0:T(8,128)S(1)}, f32[64,16,128]{2,1,0:T(8,128)S(1)}, f32[64,16,128]{2,1,0:T(8,128)S(1)}, f32[64,16,128]{2,1,0:T(8,128)S(1)}) custom-call(f32[64,16,128]{2,1,0:T(8,128)} %u_in.1, f32[64,16,128]{2,1,0:T(8,128)} %v_in.1, f32[64,16,128]{2,1,0:T(8,128)} %w_in.1, f32[64,16,128]{2,1,0:T(8,128)} %p_in.1, s32[16,128]{1,0:T(8,128)} %terr_in.1, ...), custom_call_target="tpu_custom_call" | custom-call | tf_op jit(solution)/shard_map/pallas_call | solution.py:708
  42.3 1.3 %shard_map.112 = (f32[64,16,128]{2,1,0:T(8,128)}, f32[64,16,128]{2,1,0:T(8,128)}, f32[64,16,128]{2,1,0:T(8,128)}, f32[64,16,128]{2,1,0:T(8,128)}) custom-call(f32[64,16,128]{2,1,0:T(8,128)S(1)} %get-tuple-element.8.refs_0_, f32[64,16,128]{2,1,0:T(8,128)S(1)} %get-tuple-element.9.refs_1_, f32[64,16,128]{2,1,0:T(8,128)S(1)} %get-tuple-element.10.refs_2_, ...), custom_call_target="tpu_custom_call" | custom-call | tf_op jit(solution)/shard_map/pallas_call | solution.py:717

commit v3 on v2

--- a/solution.py
+++ b/solution.py
@@ -18,8 +18,9 @@
 FU, FP, FV, FW = 0, 1, 2, 3
 LO = 8
 ROWS = 40
-PEXT = 32
+PEXT = 24
 GROUP = 16
+VMEM_LIMIT = 59 << 20
 CENT = {-3: 1.0, -2: -8.0, -1: 37.0, 0: 37.0, 1: -8.0, 2: 1.0}
 UPW = {-3: -1.0, -2: 5.0, -1: -10.0, 0: 10.0, 1: -5.0, 2: 1.0}
 
@@ -56,8 +57,13 @@
     prof_in,
     u_out,
     v_out,
-    w_out,
-    p_out,
+    wsc,
+    q_buf,
+    li,
+    wi,
+    cc,
+    keep_out,
+    gh_x,
     terr,
     zone,
     g,
@@ -65,12 +71,7 @@
     raw,
     tend,
     pres,
-    wsc,
-    q_buf,
     d_buf,
-    cc,
-    li,
-    wi,
     lhs,
     mat,
     mat_c,
@@ -89,7 +90,6 @@
     vs_y,
     vr_y,
     ub_x,
-    gh_x,
     wet_x,
     in_s,
     ini_s,
@@ -103,7 +103,6 @@
     stp_s,
     stp_r,
     hop,
-    hop_s,
     hop_r,
     fwd_s,
 ):
@@ -182,7 +181,7 @@
         return (
             raw.at[f, k, pl.ds(own, 3), :],
             raw.at[f, k, pl.ds(far, 3), :],
-            ini_s.at[d, grp],
+            ini_s.at[d],
             ini_r.at[d, grp, 0 if c is None else c],
         )
 
@@ -203,12 +202,12 @@
 
     def to_relay(d, grp):
         dst = hop.at[grp - 1, :, pl.ds(0, 3), :]
-        return ini(d, grp)[0], dst, hop_s.at[grp - 1], hop_r.at[grp - 1]
+        return ini(d, grp)[0], dst, ini_s.at[d], hop_r.at[grp - 1]
 
     def from_relay(d, grp, c=None):
         k = pl.ds(0, nz) if c is None else pl.ds(c * GROUP, GROUP)
         _, dst, _, sem = ini(d, grp, c)
-        return hop.at[grp - 1, k, pl.ds(0, 3), :], dst, fwd_s.at[grp - 1], sem
+        return hop.at[grp - 1, k, pl.ds(0, 3), :], dst, fwd_s.at[0], sem
 
     def forward(grp):
         if relay:
@@ -354,6 +353,7 @@
     rj = (lane + start_y).astype(jnp.float32)
     relax = relax_of(ci, rj)
     keep = 1.0 - relax
+    keep_out[...] = keep
     relax_hx = relax_of(
         (jnp.zeros((8, by), jnp.int32) + (start_x + bx)).astype(jnp.float32), rj[:8]
     )
@@ -544,13 +544,15 @@
 
         lax.fori_loop(0, (nz - TERRAIN_MAX) // wide, step, 0)
 
-    def substep(s, vh):
+    def halos(s, vh):
         wait_recv(SOUTH, stp(SOUTH, s))
         wait_recv(NORTH, stp(NORTH, s))
         vn_h = wet_y * (vh - (pltpu.roll(pr_y[SOUTH - 2, s], by - 1, 1) - ps_y[s]))
         vh_next = vn_h - relax_hy * (vn_h - wet_y * vb_y)
         halo = jnp.where(even, -vn_h, pltpu.roll(pr_y[NORTH - 2, s], 1, 1))
         edges_y(halo)
+        for d in range(4):
+            wait_send(d, stp(d, s))
 
         for d in (WEST, EAST):
             wait_recv(d, stp(d, s))
@@ -563,14 +565,27 @@
             first_row = pl.ds(n * bx, 8, stride=bx)
             last_row = pl.ds(n * bx + bx - 1, 8, stride=bx)
             q_buf[first_row, :] = q_buf[first_row, :] + gh * pw
-            u_out[pl.ds(n, 8), 0, :] = u_out[pl.ds(n, 8), 0, :] + keep_w * pw
             wet = wet_x[at, :]
             un = wet * (uh_x[at, :] - (pe_r[s, at, :] - pres[pl.ds(n, 8), LO + bx - 1, :]))
-            uh_x[at, :] = un - relax_hx * (un - wet * ub_x[at, :])
+            uh_x[at, :] = un
             if n < TERRAIN_MAX:
                 un = jnp.where(wet_hi, un, 0.0)
             q_buf[last_row, :] = q_buf[last_row, :] - gh * un
 
+        return vh_next
+
+    def late(s):
+        for n in range(0, nz, 8):
+            at = pl.ds(n, 8)
+            pw = pw_r[s, at, :]
+            if n < TERRAIN_MAX:
+                pw = jnp.where(wet_lo, pw, 0.0)
+            u_out[at, 0, :] = u_out[at, 0, :] + keep_w * pw
+            un = uh_x[at, :]
+            uh_x[at, :] = un - relax_hx * (un - wet_x[at, :] * ub_x[at, :])
+
+    def substep(s, vh):
+        vh_next = halos(s, vh)
         q_prev = q_buf[slab(0), :]
         x = zero
         for k in range(nz):
@@ -581,9 +596,6 @@
                 d_buf[at, :] = x
             q_prev = q
 
-        for d in (WEST, EAST):
-            wait_send(d, stp(d, s))
-
         for k in range(nz - 1, -1, -1):
             below = zero
             if k > 0:
@@ -592,67 +604,86 @@
             wsc[slab(k), :] = x * keep
             x = below
 
-        @pl.when(s < SUB - 1)
-        def _():
-            start(WEST, stp(WEST, s + 1))
-            start(EAST, stp(EAST, s + 1))
-
-        for d in (SOUTH, NORTH):
-            wait_send(d, stp(d, s))
-
-        @pl.when(s < SUB - 1)
-        def _():
-            acc = zero
-            for k in range(nz):
-                x = pltpu.roll(pres[k, pl.ds(LO, bx), :], 2 * k + 1, 1)
-                acc = jnp.where((lane >> 1) == k, x, acc)
-            ps_y[s + 1] = acc
-            start(SOUTH, stp(SOUTH, s + 1))
-            start(NORTH, stp(NORTH, s + 1))
-            over(inner)
-
+        start(WEST, stp(WEST, s + 1))
+        start(EAST, stp(EAST, s + 1))
+
+        late(s)
+        acc = zero
+        for k in range(nz):
+            x = pltpu.roll(pres[k, pl.ds(LO, bx), :], 2 * k + 1, 1)
+            acc = jnp.where((lane >> 1) == k, x, acc)
+        ps_y[s + 1] = acc
+        start(SOUTH, stp(SOUTH, s + 1))
+        start(NORTH, stp(NORTH, s + 1))
+        over(inner)
         return vh_next
 
-    lax.fori_loop(0, SUB, substep, vh0)
+    vh = lax.fori_loop(0, SUB - 1, substep, vh0)
+    halos(SUB - 1, vh)
+    late(SUB - 1)
 
     for d in (WEST, EAST):
-        wait_send(d, ini(d, 0))
-
-        @pl.when(direct(d))
-        def _(d=d):
-            for grp in (1, 2):
-                rcopy(d, *ini(d, grp)).wait_send()
+        own = pl.ds(LO if d == WEST else LO + bx - 3, 3)
+        far = pl.ds(LO + bx if d == WEST else LO - 3, 3)
+        sent = raw.at[:, :, own, :], raw.at[:, :, far, :], ini_s.at[d], ini_r.at[d, 0, 0]
+        wait_send(d, sent)
 
     if relay:
-
-        @pl.when(inner_x)
-        def _():
-            for grp in (1, 2):
-                rcopy_to(lax.rem(gx + 2, 4), *to_relay(EAST, grp)).wait_send()
 
         @pl.when(jnp.logical_not(inner_x))
         def _():
-            for grp in (1, 2):
-                rcopy_to(lax.rem(gx + 2, 4), *from_relay(EAST, grp)).wait_send()
+            src = hop.at[:, :, pl.ds(0, 3), :]
+            dst = raw.at[pl.ds(2, 2), :, pl.ds(LO - 3, 3), :]
+            rcopy_to(lax.rem(gx + 2, 4), src, dst, fwd_s.at[0], ini_r.at[0, 0, 0]).wait_send()
 
     for d in (SOUTH, NORTH):
         wait_send(d, (ys, yr.at[d - 2], iny_s.at[d - 2], iny_r.at[d - 2, 0]))
     for d in (WEST, SOUTH):
         wait_send(d, ter(d), uv(d))
 
-    def finish(k, carry):
-        w_out[k] = wsc[slab(k), :] * (1.0 / HC)
-        p_out[k] = pres[k, pl.ds(LO, bx), :] * (1.0 / HC)
-        return carry
-
-    lax.fori_loop(0, nz, finish, 0, unroll=4)
-
-
-def emit(*refs):
-    sems = refs[-1]
-    copies = [pltpu.make_async_copy(refs[n], refs[4 + n], sems.at[n]) for n in range(4)]
+
+def last(
+    nz, u, v, wsc, q, li, wi, cc, keep_ref, gh, u_out, v_out, w_out, p_out, w_buf, p_buf, d_buf, sems
+):
+    bx, by = keep_ref.shape
+    copies = [
+        pltpu.make_async_copy(u, u_out, sems.at[0]),
+        pltpu.make_async_copy(v, v_out, sems.at[1]),
+    ]
     for c in copies:
         c.start()
+    keep = keep_ref[...]
+    out = keep * (1.0 / HC)
+
+    def slab(k):
+        return pl.ds(k * bx, bx)
+
+    zero = jnp.zeros((bx, by), jnp.float32)
+    q_prev = q[slab(0), :]
+    x = zero
+    for k in range(nz):
+        at = slab(k)
+        q_next = q[slab(k + 1), :] if k < nz - 1 else zero
+        x = wi[at, :] * (wsc[at, :] - ZC * (q_next - q_prev)) + li[at, :] * x
+        if k < nz - 1:
+            d_buf[at, :] = x
+        q_prev = q_next
+
+    half = nz // 2
+    for h in (1, 0):
+        for k in range((h + 1) * half - 1, h * half - 1, -1):
+            below = zero
+            if k > 0:
+                below = d_buf[slab(k - 1), :] + cc[slab(k - 1), :] * x
+            gz = gh[pl.ds(k, 1), :] * (ZC / (HC * HC))
+            p_buf[k] = (q[slab(k), :] - gz * (x - below)) * out
+            w_buf[k] = x * out
+            x = below
+        part = pl.ds(h * half, half)
+        for n, (src, dst) in enumerate(((w_buf, w_out), (p_buf, p_out))):
+            c = pltpu.make_async_copy(src.at[part], dst.at[part], sems.at[2 + 2 * h + n])
+            c.start()
+            copies.append(c)
     for c in copies:
         c.wait()
 
@@ -679,7 +710,7 @@
             vm((4, nz, ROWS, by), f32),
             vm((4, nz * bx, by), f32),
             vm((nz, PEXT, by), f32),
-            lev, lev, lev, lev, lev, lev,
+            lev,
             vm((GROUP * bx, 4 * by), jnp.bfloat16),
             vm((4 * by, 4 * by), jnp.bfloat16),
             vm((4 * by, by), jnp.bfloat16),
@@ -693,33 +724,39 @@
             vm((SUB, nz, by), f32),
             vm((SUB, bx, by), f32),
             vm((2, SUB, bx, by), f32),
-            col, col, plane, plane, col, col, col,
+            col, col, plane, plane, col, col,
             dma((8,)),
-            dma((2, 3)), dma((2, 3, nkg)),
+            dma((2,)), dma((2, 3, nkg)),
             dma((2,)), dma((2, nkg)),
             dma((2,)), dma((2,)),
             dma((2,)), dma((2,)),
             dma((4,)), dma((4, 2)),
             vm((2, nz, 8, by), f32),
-            dma((2,)), dma((2,)), dma((2,)),
+            dma((2,)), dma((1,)),
         ]
         vspec = pl.BlockSpec(memory_space=pltpu.VMEM)
         aspec = pl.BlockSpec(memory_space=pl.ANY)
         outs = pl.pallas_call(
             functools.partial(kernel, nz, bx, cnt),
-            out_shape=[pltpu.VMEM((nz, bx, by), f32)] * 4,
-            in_specs=[aspec] * 8,
-            out_specs=[vspec] * 4,
+            out_shape=[pltpu.VMEM((nz, bx, by), f32)] * 2
+            + [pltpu.VMEM((nz * bx, by), f32)] * 5
+            + [pltpu.VMEM((bx, by), f32), pltpu.VMEM((nz, by), f32)],
+            in_specs=[pl.BlockSpec(memory_space=pltpu.HBM)] * 8,
+            out_specs=[vspec] * 9,
             scratch_shapes=scratch,
-            compiler_params=pltpu.CompilerParams(collective_id=0, has_side_effects=True),
+            compiler_params=pltpu.CompilerParams(
+                collective_id=0, has_side_effects=True, vmem_limit_bytes=VMEM_LIMIT
+            ),
         )(u, v, w, p, terr, zone, g, prof)
         outs = [pltpu.with_memory_space_constraint(a, pltpu.VMEM) for a in outs]
+        full = vm((nz, bx, by), f32)
         return pl.pallas_call(
-            emit,
+            functools.partial(last, nz),
             out_shape=[jax.ShapeDtypeStruct((nz, bx, by), f32)] * 4,
-            in_specs=[vspec] * 4,
+            in_specs=[vspec] * 9,
             out_specs=[aspec] * 4,
-            scratch_shapes=[dma((4,))],
+            scratch_shapes=[full, full, lev, dma((6,))],
+            compiler_params=pltpu.CompilerParams(vmem_limit_bytes=VMEM_LIMIT),
         )(*outs)
 
     field = P(None, "gx", "gy")

time: 43.8 us -> 43.1 us (0.984)
  Pallas kernels: 43 us -> 42.3 us
    pallas_call x1, Pallas kernels: 41.6 us -> 40.9 us  [on_device(): pl.pallas_call(functools.partial(kernel, nz, bx, cnt), out_shape=[pltpu.V...]
where the time goes in v3:
time: 43.1 us; the launch traced here: 42.9 us
  Pallas kernels  42.3 us (98%)
  between operations  0.64 us (1%)
    pallas_call x1, Pallas kernels, on_device(): pl.pallas_call(functools.partial(kernel, nz, bx, cnt), out_shape=[pltpu.V...  40.9 us
    pallas_call x1, Pallas kernels, on_device(): pl.pallas_call(functools.partial(last, nz), out_shape=[jax.ShapeDtypeStru...  1.36 us

profile of v3, /device:TPU:0, one launch (start us, length us, event | category | flops | bytes accessed | tf_op | source)
XLA Modules:
  0.0 42.9 jit_solution(7695261958056905058)
XLA Ops:
  0.6 40.9 %shard_map.111 = (f32[64,16,128]{2,1,0:T(8,128)S(1)}, f32[64,16,128]{2,1,0:T(8,128)S(1)}, f32[1024,128]{1,0:T(8,128)S(1)}, f32[1024,128]{1,0:T(8,128)S(1)}, f32[...) custom-call(f32[64,16,128]{2,1,0:T(8,128)} %u_in.1, ...), custom_call_target="tpu_custom_call" | custom-call | tf_op jit(solution)/shard_map/pallas_call | solution.py:739
  41.6 1.4 %shard_map.112 = (f32[64,16,128]{2,1,0:T(8,128)}, f32[64,16,128]{2,1,0:T(8,128)}, f32[64,16,128]{2,1,0:T(8,128)}, f32[64,16,128]{2,1,0:T(8,128)}) custom-call(f32[64,16,128]{2,1,0:T(8,128)S(1)} %get-tuple-element.13.u, f32[64,16,128]{2,1,0:T(8,128)S(1)} %get-tuple-element.14.v, f32[1024,128]{1,0:T(8,128)S(1)} %get-tuple-element.15.wsc, ...), custom_call_target="tpu_custom_call" | custom-call | tf_op jit(solution)/shard_map/pallas_call | solution.py:753

commit v4 on v3

--- a/solution.py
+++ b/solution.py
@@ -133,17 +133,21 @@
         greet({"gx": lax.rem(gx + 2, 4)})
 
     loads = [
-        pltpu.make_async_copy(src, raw.at[f, :, pl.ds(LO, bx), :], in_s.at[f])
+        pltpu.make_async_copy(src, raw.at[f, :, pl.ds(LO, bx), :], in_s.at[f // 2])
         for f, src in ((FU, u_in), (FP, p_in), (FV, v_in), (FW, w_in))
     ]
     small = [
-        pltpu.make_async_copy(src, dst, in_s.at[4 + n])
+        pltpu.make_async_copy(src, dst, in_s.at[2 + n])
         for n, (src, dst) in enumerate(
             ((terr_in, terr), (zone_in, zone), (g_in, g), (prof_in, prof))
         )
     ]
     for c in loads + small:
         c.start()
+
+    def loaded(n):
+        pair = raw.at[pl.ds(2 * n, 2), :, pl.ds(LO, bx), :]
+        pltpu.make_async_copy(pair, pair, in_s.at[n]).wait()
 
     def rcopy(d, src, dst, ss, rs):
         return pltpu.make_async_remote_copy(
@@ -173,16 +177,18 @@
             for c in copies:
                 rcopy(d, *c).wait_recv()
 
+    blocks = (nkg, nkg // 2, nkg)
+
     def ini(d, grp, c=None):
         own = LO if d == WEST else LO + bx - 3
         far = LO + bx if d == WEST else LO - 3
         f = pl.ds(0, 2) if grp == 0 else grp + 1
-        k = pl.ds(0, nz) if c is None else pl.ds(c * GROUP, GROUP)
+        k = pl.ds(0, nz) if c is None else pl.ds(c * (nz // blocks[grp]), nz // blocks[grp])
         return (
             raw.at[f, k, pl.ds(own, 3), :],
             raw.at[f, k, pl.ds(far, 3), :],
             ini_s.at[d],
-            ini_r.at[d, grp, 0 if c is None else c],
+            ini_r.at[d, sum(blocks[:grp]) + (0 if c is None else c)],
         )
 
     def direct(d):
@@ -205,7 +211,7 @@
         return ini(d, grp)[0], dst, ini_s.at[d], hop_r.at[grp - 1]
 
     def from_relay(d, grp, c=None):
-        k = pl.ds(0, nz) if c is None else pl.ds(c * GROUP, GROUP)
+        k = pl.ds(0, nz) if c is None else pl.ds(c * (nz // blocks[grp]), nz // blocks[grp])
         _, dst, _, sem = ini(d, grp, c)
         return hop.at[grp - 1, k, pl.ds(0, 3), :], dst, fwd_s.at[0], sem
 
@@ -216,7 +222,7 @@
                 @pl.when(gx == at)
                 def _(d=d):
                     rcopy_to(lax.rem(gx + 2, 4), *to_relay(d, grp)).wait_recv()
-                    for c in range(nkg):
+                    for c in range(blocks[grp]):
                         rcopy_to((gx + 1, gx - 1)[d == EAST], *from_relay(d, grp, c)).start()
 
     def start_direct(grp):
@@ -224,7 +230,7 @@
 
             @pl.when(direct(d))
             def _(d=d):
-                for c in range(nkg):
+                for c in range(blocks[grp]):
                     rcopy(d, *ini(d, grp, c)).start()
 
     def iny(d, c):
@@ -289,15 +295,13 @@
                 vr_y[...] = jnp.zeros(vr_y.shape, jnp.float32)
 
     small[0].wait()
-    loads[0].wait()
-    loads[1].wait()
+    loaded(0)
     pl.semaphore_wait(barrier, sum(h.astype(jnp.int32) for h in has) + int(relay))
     start(WEST, ter(WEST))
     start(SOUTH, ter(SOUTH))
     for d in (WEST, EAST):
         start(d, *[ini(d, 0, c) for c in range(nkg)])
-    loads[2].wait()
-    loads[3].wait()
+    loaded(1)
     if relay:
         for d, at in ((EAST, 1), (WEST, 2)):
 
@@ -502,7 +506,8 @@
 
     acc = zero
     for c in range(nkg):
-        wait_ini(1, c)
+        if c % 2 == 0:
+            wait_ini(1, c // 2)
         acc = lax.fori_loop(c * GROUP, (c + 1) * GROUP, second, acc, unroll=4)
         if c == 0:
             inner(0, TERRAIN_MAX, True)
@@ -625,7 +630,7 @@
     for d in (WEST, EAST):
         own = pl.ds(LO if d == WEST else LO + bx - 3, 3)
         far = pl.ds(LO + bx if d == WEST else LO - 3, 3)
-        sent = raw.at[:, :, own, :], raw.at[:, :, far, :], ini_s.at[d], ini_r.at[d, 0, 0]
+        sent = raw.at[:, :, own, :], raw.at[:, :, far, :], ini_s.at[d], ini_r.at[d, 0]
         wait_send(d, sent)
 
     if relay:
@@ -634,7 +639,7 @@
         def _():
             src = hop.at[:, :, pl.ds(0, 3), :]
             dst = raw.at[pl.ds(2, 2), :, pl.ds(LO - 3, 3), :]
-            rcopy_to(lax.rem(gx + 2, 4), src, dst, fwd_s.at[0], ini_r.at[0, 0, 0]).wait_send()
+            rcopy_to(lax.rem(gx + 2, 4), src, dst, fwd_s.at[0], ini_r.at[0, 0]).wait_send()
 
     for d in (SOUTH, NORTH):
         wait_send(d, (ys, yr.at[d - 2], iny_s.at[d - 2], iny_r.at[d - 2, 0]))
@@ -725,8 +730,8 @@
             vm((SUB, bx, by), f32),
             vm((2, SUB, bx, by), f32),
             col, col, plane, plane, col, col,
-            dma((8,)),
-            dma((2,)), dma((2, 3, nkg)),
+            dma((6,)),
+            dma((2,)), dma((2, 2 * nkg + nkg // 2)),
             dma((2,)), dma((2, nkg)),
             dma((2,)), dma((2,)),
             dma((2,)), dma((2,)),

time: 43.1 us -> 43 us (level)
  no operation moved by 1% of the time
where the time goes in v4:
time: 43 us; the launch traced here: 42.9 us
  Pallas kernels  42.2 us (98%)
  between operations  0.64 us (1%)
    pallas_call x1, Pallas kernels, on_device(): pl.pallas_call(functools.partial(kernel, nz, bx, cnt), out_shape=[pltpu.V...  40.9 us
    pallas_call x1, Pallas kernels, on_device(): pl.pallas_call(functools.partial(last, nz), out_shape=[jax.ShapeDtypeStru...  1.36 us

profile of v4, /device:TPU:0, one launch (start us, length us, event | category | flops | bytes accessed | tf_op | source)
XLA Modules:
  0.0 42.9 jit_solution(14196310440423510316)
XLA Ops:
  0.6 40.9 %shard_map.111 = (f32[64,16,128]{2,1,0:T(8,128)S(1)}, f32[64,16,128]{2,1,0:T(8,128)S(1)}, f32[1024,128]{1,0:T(8,128)S(1)}, f32[1024,128]{1,0:T(8,128)S(1)}, f32[...) custom-call(f32[64,16,128]{2,1,0:T(8,128)} %u_in.1, ...), custom_call_target="tpu_custom_call" | custom-call | tf_op jit(solution)/shard_map/pallas_call | solution.py:744
  41.5 1.4 %shard_map.112 = (f32[64,16,128]{2,1,0:T(8,128)}, f32[64,16,128]{2,1,0:T(8,128)}, f32[64,16,128]{2,1,0:T(8,128)}, f32[64,16,128]{2,1,0:T(8,128)}) custom-call(f32[64,16,128]{2,1,0:T(8,128)S(1)} %get-tuple-element.13.u, f32[64,16,128]{2,1,0:T(8,128)S(1)} %get-tuple-element.14.v, f32[1024,128]{1,0:T(8,128)S(1)} %get-tuple-element.15.wsc, ...), custom_call_target="tpu_custom_call" | custom-call | tf_op jit(solution)/shard_map/pallas_call | solution.py:758
